TPU v7x, 32 devices: a whole 2x2x4 slice. The times are simulated.
32 devices in a mesh: ctx: 8 (over z, x), tp: 4 (over y, core).
Axes of the slice: x: 2, y: 2, z: 4, core: 2. Of those that a mesh axis runs over, the one named last changes fastest.
Arguments:
- hidden_in: bfloat16 [4096, 5376], P(('ctx', 'tp')), may hold values from -6 to 6
- stretch_start: int32 [1], replicated, may hold values from 1 to 1024
- pre_gain: float32 [5376], replicated, may hold values from 0.1 to 1.9
- q_weight: bfloat16 [5376, 4096], P('ctx', 'tp'), may hold values from -1 to 1
- k_weight: bfloat16 [5376, 2048], P('ctx', 'tp'), may hold values from -1 to 1
- v_weight: bfloat16 [5376, 2048], P('ctx', 'tp'), may hold values from -0.078125 to 0.078125
- o_weight: bfloat16 [4096, 5376], P('tp', 'ctx'), may hold values from -0.09375 to 0.09375
- q_gain: float32 [128], replicated, may hold values from 0.5 to 5
- k_gain: float32 [128], replicated, may hold values from 0.5 to 5
- prior_keys: bfloat16 [1024, 2048], P(None, 'tp'), may hold values from -6 to 6
- prior_values: bfloat16 [1024, 2048], P(None, 'tp'), may hold values from -6 to 6
- post_gain: float32 [5376], replicated, may hold values from 0.1 to 1.9
Outputs:
- result: bfloat16 [4096, 5376], P(('ctx', 'tp'))
All inputs are finite; a program needn't handle non-finite values.
Results may differ from a plain program's by a relative error of at most 0.013.
Values may be sent and summed in bfloat16 or wider, within the bound.
No kernel may reach another device: no remote copies, remote signals or barrier semaphores. Data moves between devices by JAX's collectives and lax.ppermute only.
A program may use at most 128 MiB of HBM per device.

v0:
```python
import jax
import jax.numpy as jnp
from jax import lax
from jax.sharding import PartitionSpec as P

HD = 128
WINDOW = 1024
EPSILON = 1e-06
QUERY_FACTOR = 168.0 ** (-0.5)


def from_behind(value, axis, steps):
    count = lax.axis_size(axis)
    leading, last = (max(0, -steps), min(count, count - steps))
    return lax.ppermute(value, axis, [(source, source + steps) for source in range(leading, last)])


def rms_scale(inputs, scales):
    mean_sq = jnp.mean(inputs * inputs, axis=-1, keepdims=True)
    return inputs * lax.rsqrt(mean_sq + EPSILON) * scales


def rotate(inputs, positions):
    half_dim = inputs.shape[-1] // 2
    frequency = 10000.0 ** (-jnp.arange(half_dim, dtype=jnp.float32) / half_dim)
    angles = positions.astype(jnp.float32)[:, None] * frequency[None, :]
    cosines = jnp.cos(angles)[:, None, :]
    sines = jnp.sin(angles)[:, None, :]
    front = inputs[..., :half_dim]
    second = inputs[..., half_dim:]
    return jnp.concatenate(
        [front * cosines - second * sines, second * cosines + front * sines], axis=-1
    )


def local(
    hidden_in,
    stretch_start,
    pre_gain,
    q_weight,
    k_weight,
    v_weight,
    o_weight,
    q_gain,
    k_gain,
    prior_keys,
    prior_values,
    post_gain,
):
    residual_in = hidden_in.astype(jnp.float32)
    normed = rms_scale(residual_in, pre_gain).astype(jnp.bfloat16)
    block_rows = lax.all_gather(normed, "tp", axis=0, tiled=True)
    row_count = block_rows.shape[0]
    query_cols = q_weight.shape[1]
    kv_cols = k_weight.shape[1]

    def add_piece(segment):
        return jnp.dot(block_rows, segment, preferred_element_type=jnp.float32)

    query_raw = add_piece(lax.all_gather(q_weight, "ctx", axis=0, tiled=True))
    key_raw = add_piece(lax.all_gather(k_weight, "ctx", axis=0, tiled=True))
    value_raw = add_piece(lax.all_gather(v_weight, "ctx", axis=0, tiled=True))
    local_heads = query_cols // HD
    local_kv = kv_cols // HD
    group = local_heads // local_kv
    chain_pos = lax.axis_index("ctx")
    positions = WINDOW + chain_pos * row_count + jnp.arange(row_count, dtype=jnp.int32)
    query = (
        rotate(rms_scale(query_raw.reshape(row_count, local_heads, HD), q_gain), positions)
        * QUERY_FACTOR
    ).astype(jnp.bfloat16)
    key_rows = (
        rotate(rms_scale(key_raw.reshape(row_count, local_kv, HD), k_gain), positions)
        .astype(jnp.bfloat16)
        .reshape(row_count, kv_cols)
    )
    value_rows = value_raw.astype(jnp.bfloat16)
    reach = WINDOW // row_count
    earlier = [
        from_behind((key_rows, value_rows), "ctx", hop_index + 1) for hop_index in range(reach)
    ]
    key_parts = []
    value_parts = []
    for hop_index in range(reach - 1, -1, -1):
        source = chain_pos - (hop_index + 1)
        offset = jnp.maximum(WINDOW + source * row_count, 0)
        cached_keys = lax.dynamic_slice_in_dim(prior_keys, offset, row_count, 0)
        cached_values = lax.dynamic_slice_in_dim(prior_values, offset, row_count, 0)
        key_parts.append(jnp.where(source < 0, cached_keys, earlier[hop_index][0]))
        value_parts.append(jnp.where(source < 0, cached_values, earlier[hop_index][1]))
    key_parts.append(key_rows)
    value_parts.append(value_rows)
    span = (reach + 1) * row_count
    all_keys = jnp.concatenate(key_parts, axis=0).reshape(span, local_kv, HD)
    all_values = jnp.concatenate(value_parts, axis=0).reshape(span, local_kv, HD)
    key_anchor = WINDOW + (chain_pos - reach) * row_count
    query_grouped = query.reshape(row_count, local_kv, group, HD)
    scores = jnp.einsum(
        "qhgd,khd->hgqk", query_grouped, all_keys, preferred_element_type=jnp.float32
    )
    key_pos = key_anchor + jnp.arange(span, dtype=jnp.int32)
    first_valid = WINDOW - stretch_start[0]
    allowed = (
        (key_pos[None, :] <= positions[:, None])
        & (key_pos[None, :] > positions[:, None] - WINDOW)
        & (key_pos[None, :] >= first_valid)
    )
    scores = jnp.where(allowed[None, None, :, :], scores, jnp.float32(-1e30))
    largest = jnp.max(scores, axis=-1, keepdims=True)
    expon = jnp.exp(scores - largest)
    attn_probs = (expon / jnp.sum(expon, axis=-1, keepdims=True)).astype(jnp.bfloat16)
    attended = jnp.einsum(
        "hgqk,khd->qhgd", attn_probs, all_values, preferred_element_type=jnp.float32
    )
    attended = attended.astype(jnp.bfloat16).reshape(row_count, query_cols)
    partial_rows = jnp.dot(
        attended,
        lax.all_gather(o_weight, "ctx", axis=1, tiled=True),
        preferred_element_type=jnp.float32,
    )
    summed = lax.psum_scatter(
        partial_rows.astype(jnp.bfloat16), "tp", scatter_dimension=0, tiled=True
    ).astype(jnp.float32)
    return (residual_in + rms_scale(summed, post_gain)).astype(jnp.bfloat16)


def solution(mesh):
    return jax.shard_map(
        local,
        mesh=mesh,
        in_specs=(
            P(("ctx", "tp"), None),
            P(),
            P(),
            P("ctx", "tp"),
            P("ctx", "tp"),
            P("ctx", "tp"),
            P("tp", "ctx"),
            P(),
            P(),
            P(None, "tp"),
            P(None, "tp"),
            P(),
        ),
        out_specs=P(("ctx", "tp"), None),
        check_vma=False,
    )
```

profile of v0, /device:TPU:0, one launch (start us, length us, event | category | flops | bytes accessed | tf_op | source)
XLA Modules:
  0.0 664.7 jit_solution(9965920459729933018)
XLA Ops:
  6.5 1.7 fusion.9
  8.2 2.8 fusion.11
  14.5 1.0 multiply_cosine_fusion
  15.5 1.9 and_and_fusion
  17.4 38.5 %all-gather.6.cloned.1.call-done = bf16[512,5376]{1,0:T(8,128)(2,1)} async-done(((bf16[128,5376]{1,0:T(8,128)(2,1)}), bf16[512,5376]{1,0:T(8,128)(2,1)}) %all-gather.6.cloned.1.call-update) | async-done | bytes 5505040 | tf_op jit(solution)/shard_map/all_gather | solution.py:52
  55.8 91.3 %all-gather.8.cloned.1.call-done = bf16[5376,512]{1,0:T(8,128)(2,1)} async-done(((bf16[672,512]{1,0:T(8,128)(2,1)}), bf16[5376,512]{1,0:T(8,128)(2,1)}) %all-gather.8.cloned.1.call-update) | async-done | bytes 5505040 | tf_op jit(solution)/shard_map/all_gather | solution.py:62
  147.2 8.0 %convolution_convert_fusion.1 = bf16[512,512]{1,0:T(8,128)(2,1)} fusion(bf16[512,5376]{1,0:T(8,128)(2,1)} %all-gather.6.cloned.1.call-done, bf16[5376,512]{1,0:T(8,128)(2,1)} %all-gather.8.cloned.1.call-done), kind=kOutput, calls=%fused_computation.32 | convolution fusion | flops 2818834432 | bytes 11534336 | tf_op jit(solution)/shard_map/dot_general | solution.py:58
  155.2 3.4 collective-permute-start
  158.6 3.3 collective-permute-start.1
  161.8 93.2 %all-gather.10.cloned.1.call-done = bf16[5376,512]{1,0:T(8,128)(2,1)} async-done(((bf16[672,512]{1,0:T(8,128)(2,1)}), bf16[5376,512]{1,0:T(8,128)(2,1)}) %all-gather.10.cloned.1.call-update) | async-done | bytes 5505040 | tf_op jit(solution)/shard_map/all_gather | solution.py:61
  255.0 6.7 %multiply_reduce_fusion.1 = (f32[512,4]{0,1:T(4,128)S(1)}, f32[512,512]{0,1:T(8,128)S(1)}) fusion(bf16[512,5376]{1,0:T(8,128)(2,1)} %all-gather.6.cloned.1.call-done, bf16[5376,512]{1,0:T(8,128)(2,1)} %all-gather.10.cloned.1.call-done), kind=kOutput, calls=%fused_computation.37 | convolution fusion | flops 2819094528 | bytes 12066816 | tf_op jit(solution)/shard_map/dot_general | solution.py:58
  263.2 3.2 collective-permute-start.2
  266.4 3.2 collective-permute-start.3
  270.4 1.1 pad_maximum_fusion
  271.6 1.6 copy.43
  273.2 14.0 %collective-permute-done.2 = bf16[512,512]{1,0:T(8,128)(2,1)} collective-permute-done((bf16[512,512]{1,0:T(8,128)(2,1)S(1)}, bf16[512,512]{1,0:T(8,128)(2,1)}, u32[]{:S(2)}, u32[]{:S(2)}) %collective-permute-start.2) | collective-permute-done | bytes 524320 | tf_op jit(solution)/shard_map/ppermute | solution.py:15
  287.2 3.3 collective-permute-done.3
  290.5 1.6 select_bitcast_fusion.1
  292.1 0.9 copy.51
  293.0 0.9 copy.52
  293.9 138.7 %all-gather.12.cloned.1.call-done = bf16[5376,1024]{1,0:T(8,128)(2,1)} async-done(((bf16[672,1024]{1,0:T(8,128)(2,1)}), bf16[5376,1024]{1,0:T(8,128)(2,1)}) %all-gather.12.cloned.1.call-update) | async-done | bytes 11010064 | tf_op jit(solution)/shard_map/all_gather | solution.py:60
  432.6 10.2 %convolution_bitcast_fusion = f32[64,8,8,128]{3,1,2,0:T(8,128)S(1)} fusion(bf16[512,5376]{1,0:T(8,128)(2,1)} %all-gather.6.cloned.1.call-done, bf16[5376,1024]{1,0:T(8,128)(2,1)} %all-gather.12.cloned.1.call-done), kind=kOutput, calls=%fused_computation.28 | convolution fusion | flops 5637144576 | bytes 18612224 | tf_op jit(solution)/shard_map/dot_general | solution.py:58
  444.2 0.9 multiply_multiply_fusion
  445.1 1.1 multiply_subtract_fusion
  448.2 11.9 %fusion.15 = f32[4,1536,512,2]{2,1,3,0:T(8,128)} fusion(bf16[512,4,2,128]{3,0,2,1:T(8,128)(2,1)S(1)} %fusion.13, bf16[512,4,128]{2,0,1:T(8,128)(2,1)S(1)} %maximum_convert_fusion, bf16[512,4,128]{2,0,1:T(8,128)(2,1)S(1)} %bitcast.68, bf16[512,4,128]{2,0,1:T(8,128)(2,1)S(1)} %bitcast.70), kind=kOutput, calls=%fused_computation.38 | convolution fusion | flops 1615331328 | bytes 27787264 | tf_op jit(solution)/shard_map/qhgd,khd->hgqk/dot_general | solution.py:98
  460.1 7.9 %fusion.25 = f32[4,2,512]{2,1,0:T(2,128)S(1)} fusion(pred[512,1536]{0,1:T(8,128)(4,1)S(1)} %copy-done.4, bf16[512,4,2,128]{3,0,2,1:T(8,128)(2,1)S(1)} %fusion.13, bf16[512,4,128]{2,0,1:T(8,128)(2,1)S(1)} %maximum_convert_fusion, bf16[512,4,128]{2,0,1:T(8,128)(2,1)S(1)} %bitcast.69, bf16[512,4,128]{2,0,1:T(8,128)(2,1)S(1)} %bitcast.71), kind=kOutput, calls=%fused_computation.63 | convolution fusion | flops 1634207232 | bytes 3424256 | tf_op jit(solution)/shard_map/sub | solution.py:110
  468.0 13.2 %fusion.14 = bf16[4,128,2,512]{3,1,2,0:T(8,128)(2,1)S(1)} fusion(bf16[1536,4,128,1]{0,2,3,1:T(8,128)(2,1)} %bitcast.72, f32[4,2,512]{2,1,0:T(2,128)S(1)} %fusion.25, f32[4,1536,512,2]{2,1,3,0:T(8,128)} %fusion.15, pred[512,1536]{0,1:T(8,128)(4,1)S(1)} %copy-done.4), kind=kOutput, calls=%fused_computation.31 | convolution fusion | flops 1636308480 | bytes 28590080 | tf_op jit(solution)/shard_map/hgqk,khd->qhgd/dot_general | solution.py:112
  481.2 108.6 %all-gather.14.cloned.1.call-done = bf16[1024,5376]{0,1:T(8,128)(2,1)} async-done(((bf16[1024,672]{0,1:T(8,128)(2,1)}), bf16[1024,5376]{0,1:T(8,128)(2,1)}) %all-gather.14.cloned.1.call-update) | async-done | bytes 11010064 | tf_op jit(solution)/shard_map/all_gather | solution.py:118
  589.8 12.0 %convolution_convert_fusion = bf16[512,5376]{1,0:T(8,128)(2,1)} fusion(bf16[512,1024]{0,1:T(8,128)(2,1)S(1)} %bitcast.74, bf16[1024,5376]{0,1:T(8,128)(2,1)} %all-gather.14.cloned.1.call-done), kind=kOutput, calls=%fused_computation.8 | convolution fusion | flops 5639897088 | bytes 17563648 | tf_op jit(solution)/shard_map/dot_general | solution.py:116
  601.8 51.4 %reduce-scatter.2.cloned.1.call-done = bf16[128,5376]{1,0:T(8,128)(2,1)} async-done(((bf16[512,5376]{1,0:T(8,128)(2,1)}), bf16[128,5376]{1,0:T(8,128)(2,1)}) %reduce-scatter.2.cloned.1.call-update) | async-done | bytes 1376272 | tf_op jit(solution)/shard_map/reduce_scatter | solution.py:121
  653.2 1.7 fusion.7
  654.9 3.0 fusion.12
  (52 shorter events, 8.1 us)
Async XLA Ops:
  6.5 49.3 %all-gather.6.cloned.1.call-start = ((), (), s32[]{:S(2)}) async-start(), calls=%async_computation.1 | async-start | bytes 6881280 | tf_op jit(solution)/shard_map/all_gather | solution.py:52
  11.1 136.1 %all-gather.8.cloned.1.call-start = ((), (), s32[]{:S(2)}) async-start(), calls=%async_computation.2 | async-start | bytes 6193152 | tf_op jit(solution)/shard_map/all_gather | solution.py:62
  11.8 243.2 %all-gather.10.cloned.1.call-start = ((), (), s32[]{:S(2)}) async-start(), calls=%async_computation.3 | async-start | bytes 6193152 | tf_op jit(solution)/shard_map/all_gather | solution.py:61
  12.6 420.0 %all-gather.12.cloned.1.call-start = ((), (), s32[]{:S(2)}) async-start(), calls=%async_computation.4 | async-start | bytes 12386304 | tf_op jit(solution)/shard_map/all_gather | solution.py:60
  13.1 576.6 %all-gather.14.cloned.1.call-start = ((), (), s32[]{:S(2)}) async-start(), calls=%async_computation.5 | async-start | bytes 12386304 | tf_op jit(solution)/shard_map/all_gather | solution.py:118
  13.7 639.4 %reduce-scatter.2.cloned.1.call-start = ((), (), s32[]{:S(2)}) async-start(), calls=%async_computation.6 | async-start | bytes 6881280 | tf_op jit(solution)/shard_map/reduce_scatter | solution.py:121
  155.2 106.9 %copy-start.6 = (f32[128]{0:T(128)S(1)}, f32[128]{0:T(128)}, u32[]{:S(2)}) copy-start(f32[128]{0:T(128)} %param.20) | copy-start | bytes 1540
  155.2 114.8 %collective-permute-start = (bf16[512,512]{1,0:T(8,128)(2,1)}, bf16[512,512]{1,0:T(8,128)(2,1)}, u32[]{:S(2)}, u32[]{:S(2)}) collective-permute-start(bf16[512,512]{1,0:T(8,128)(2,1)} %convolution_convert_fusion.1), channel_id=1, source_target_pairs={{0,8},{4,12},{8,16},{12,20},{16,24},{20,28},{1,9},{5,13},{9,17},{1... | collective-permute-start | bytes 1572872 | tf_op jit(solution)/shard_map/ppermute | solution.py:15
  158.6 111.4 %collective-permute-start.1 = (bf16[512,512]{1,0:T(8,128)(2,1)}, bf16[512,512]{1,0:T(8,128)(2,1)}, u32[]{:S(2)}, u32[]{:S(2)}) collective-permute-start(bf16[512,512]{1,0:T(8,128)(2,1)} %convolution_convert_fusion.1), channel_id=1, source_target_pairs={{0,4},{4,8},{8,12},{12,16},{16,20},{20,24},{24,28},{1,5},{5,9},{9,... | collective-permute-start | bytes 1572872 | tf_op jit(solution)/shard_map/ppermute | solution.py:15
  262.4 7.6 %copy-start.3 = (bf16[1024,512]{1,0:T(8,128)(2,1)S(1)}, bf16[1024,512]{1,0:T(8,128)(2,1)}, u32[]{:S(2)}) copy-start(bf16[1024,512]{1,0:T(8,128)(2,1)} %param.22) | copy-start | bytes 3145732
  263.2 24.0 %collective-permute-start.2 = (bf16[512,512]{1,0:T(8,128)(2,1)S(1)}, bf16[512,512]{1,0:T(8,128)(2,1)}, u32[]{:S(2)}, u32[]{:S(2)}) collective-permute-start(bf16[512,512]{1,0:T(8,128)(2,1)S(1)} %copy_bitcast_fusion), channel_id=1, source_target_pairs={{0,8},{4,12},{8,16},{12,20},{16,24},{20,28},{1,9},{5,13},{9,17},{1... | collective-permute-start | bytes 1572872 | tf_op jit(solution)/shard_map/ppermute | solution.py:15
  266.4 24.1 %collective-permute-start.3 = (bf16[512,512]{1,0:T(8,128)(2,1)S(1)}, bf16[512,512]{1,0:T(8,128)(2,1)}, u32[]{:S(2)}, u32[]{:S(2)}) collective-permute-start(bf16[512,512]{1,0:T(8,128)(2,1)S(1)} %copy_bitcast_fusion), channel_id=1, source_target_pairs={{0,4},{4,8},{8,12},{12,16},{16,20},{20,24},{24,28},{1,5},{5,9},{9,... | collective-permute-start | bytes 1572872 | tf_op jit(solution)/shard_map/ppermute | solution.py:15
  442.8 1.4 copy-start.7
  447.0 1.0 copy-start.1
  447.0 1.2 copy-start.2
  448.2 11.9 %copy-start.4 = (pred[512,1536]{0,1:T(8,128)(4,1)S(1)}, pred[512,1536]{0,1:T(8,128)(4,1)}, u32[]{:S(2)}) copy-start(pred[512,1536]{0,1:T(8,128)(4,1)} %and_and_fusion) | copy-start | bytes 2359300
  601.8 53.1 %copy-start = (bf16[128,5376]{1,0:T(8,128)(2,1)S(1)}, bf16[128,5376]{1,0:T(8,128)(2,1)}, u32[]{:S(2)}) copy-start(bf16[128,5376]{1,0:T(8,128)(2,1)} %param.12) | copy-start | bytes 4128772
  601.8 53.1 %copy-start.5 = (f32[5376]{0:T(1024)S(1)}, f32[5376]{0:T(1024)}, u32[]{:S(2)}) copy-start(f32[5376]{0:T(1024)} %param.23) | copy-start | bytes 64516
Sparse Core Ops, SparseCore 0:
  11.2 44.6 all-gather.5
  58.0 89.1 all-gather.7
  149.4 105.6 all-gather.9
  257.0 175.5 all-gather.11
  434.6 155.0 all-gather.13
  601.9 51.2 reduce-scatter.1
where the time goes:
time: 665 us
  waiting for transfers between devices  541 us (81%)
  matrix products  69.9 us (11%)
  other arithmetic  19.8 us (3%)
  between operations  14.4 us (2%)
  starting transfers between devices  13.4 us (2%)
    all_gather x1, waiting for transfers between devices, local(): query_raw = add_piece(lax.all_gather(q_weight, 'ctx', axis=0, tiled=True))  139 us
    all_gather x1, waiting for transfers between devices, local(): lax.all_gather(o_weight, 'ctx', axis=1, tiled=True)  109 us
    all_gather x1, waiting for transfers between devices, local(): key_raw = add_piece(lax.all_gather(k_weight, 'ctx', axis=0, tiled=True))  93.2 us
    all_gather x1, waiting for transfers between devices, local(): value_raw = add_piece(lax.all_gather(v_weight, 'ctx', axis=0, tiled=True))  91.3 us
    reduce_scatter x1, waiting for transfers between devices, local(): lax.psum_scatter(partial_rows.astype(jnp.bfloat16), 'tp', scatter_dimensi...  51.4 us
    all_gather x1, waiting for transfers between devices, local(): block_rows = lax.all_gather(normed, 'tp', axis=0, tiled=True)  38.5 us
    dot_general x3, matrix products, add_piece(): return jnp.dot(block_rows, segment, preferred_element_type=jnp.float32)  24.9 us
    ppermute x4, waiting for transfers between devices, from_behind(): lax.ppermute(value, axis, [(source, source + steps) for source in range(l...  17.3 us
  transfers between devices with their start and end apart: 10, of which 8 were waited for; matrix products, arithmetic and copies ran while one was open for 11% of the time, Pallas kernels for 0%

commit v1 on v0

--- a/solution.py
+++ b/solution.py
@@ -115,7 +115,7 @@
     attended = attended.astype(jnp.bfloat16).reshape(row_count, query_cols)
     partial_rows = jnp.dot(
         attended,
-        lax.all_gather(o_weight, "ctx", axis=1, tiled=True),
+        jnp.concatenate(lax.all_gather(o_weight, "ctx"), axis=1),
         preferred_element_type=jnp.float32,
     )
     summed = lax.psum_scatter(

time: 665 us -> 697 us (1.048)
  local copies, waits for them, and re-layouts: 5.81 us -> 24.5 us
  waiting for transfers between devices: 541 us -> 555 us
    all_gather x1, waiting for transfers between devices: 109 us -> 122 us  [local(): lax.all_gather(o_weight, 'ctx')]
    unnamed x17 -> x20, local copies, waits for them, and re-layouts: 1.07 us -> 11.9 us
    reshape x0 -> x1, local copies, waits for them, and re-layouts: none -> 7.85 us  [local(): jnp.concatenate(lax.all_gather(o_weight, 'ctx'), axis=1)]
  transfers between devices with their start and end apart: 10 -> 10, of which waited for: 8 -> 8; matrix products, arithmetic and copies ran while one was open for 11% -> 9% of each run, Pallas kernels for 0% -> 0%
where the time goes in v1:
time: 697 us; the launch traced here: 696 us
  waiting for transfers between devices  555 us (80%)
  matrix products  69.7 us (10%)
  local copies, waits for them, and re-layouts  24.5 us (4%)
  other arithmetic  19.8 us (3%)
  between operations  14.4 us (2%)
  starting transfers between devices  13.4 us (2%)
    all_gather x1, waiting for transfers between devices, local(): query_raw = add_piece(lax.all_gather(q_weight, 'ctx', axis=0, tiled=True))  139 us
    all_gather x1, waiting for transfers between devices, local(): lax.all_gather(o_weight, 'ctx')  122 us
    all_gather x1, waiting for transfers between devices, local(): key_raw = add_piece(lax.all_gather(k_weight, 'ctx', axis=0, tiled=True))  93.2 us
    all_gather x1, waiting for transfers between devices, local(): value_raw = add_piece(lax.all_gather(v_weight, 'ctx', axis=0, tiled=True))  91.3 us
    reduce_scatter x1, waiting for transfers between devices, local(): lax.psum_scatter(partial_rows.astype(jnp.bfloat16), 'tp', scatter_dimensi...  51.4 us
    all_gather x1, waiting for transfers between devices, local(): block_rows = lax.all_gather(normed, 'tp', axis=0, tiled=True)  38.5 us
    dot_general x3, matrix products, add_piece(): return jnp.dot(block_rows, segment, preferred_element_type=jnp.float32)  24.9 us
    ppermute x4, waiting for transfers between devices, from_behind(): lax.ppermute(value, axis, [(source, source + steps) for source in range(l...  17.3 us
  transfers between devices with their start and end apart: 10, of which 8 were waited for; matrix products, arithmetic and copies ran while one was open for 9% of the time, Pallas kernels for 0%

profile of v1, /device:TPU:0, one launch (start us, length us, event | category | flops | bytes accessed | tf_op | source)
XLA Modules:
  0.0 696.4 jit_solution(17433707496782265967)
XLA Ops:
  6.5 1.7 fusion.9
  8.2 2.8 fusion.11
  14.5 1.0 multiply_cosine_fusion
  15.5 1.9 and_and_fusion
  17.4 38.5 %all-gather.7.cloned.1.call-done = bf16[512,5376]{1,0:T(8,128)(2,1)} async-done(((bf16[128,5376]{1,0:T(8,128)(2,1)}), bf16[512,5376]{1,0:T(8,128)(2,1)}) %all-gather.7.cloned.1.call-update) | async-done | bytes 5505040 | tf_op jit(solution)/shard_map/all_gather | solution.py:52
  55.8 91.3 %all-gather.9.cloned.1.call-done = bf16[5376,512]{1,0:T(8,128)(2,1)} async-done(((bf16[672,512]{1,0:T(8,128)(2,1)}), bf16[5376,512]{1,0:T(8,128)(2,1)}) %all-gather.9.cloned.1.call-update) | async-done | bytes 5505040 | tf_op jit(solution)/shard_map/all_gather | solution.py:62
  147.2 8.0 %convolution_convert_fusion.1 = bf16[512,512]{1,0:T(8,128)(2,1)} fusion(bf16[512,5376]{1,0:T(8,128)(2,1)} %all-gather.7.cloned.1.call-done, bf16[5376,512]{1,0:T(8,128)(2,1)} %all-gather.9.cloned.1.call-done), kind=kOutput, calls=%fused_computation.32 | convolution fusion | flops 2818834432 | bytes 11534336 | tf_op jit(solution)/shard_map/dot_general | solution.py:58
  155.2 3.4 collective-permute-start
  158.6 3.3 collective-permute-start.1
  161.8 93.2 %all-gather.11.cloned.1.call-done = bf16[5376,512]{1,0:T(8,128)(2,1)} async-done(((bf16[672,512]{1,0:T(8,128)(2,1)}), bf16[5376,512]{1,0:T(8,128)(2,1)}) %all-gather.11.cloned.1.call-update) | async-done | bytes 5505040 | tf_op jit(solution)/shard_map/all_gather | solution.py:61
  255.0 6.7 multiply_reduce_fusion.1
  263.2 3.3 collective-permute-start.2
  266.4 3.3 collective-permute-start.3
  270.4 1.1 pad_maximum_fusion
  271.6 1.6 copy.62
  273.2 14.0 %collective-permute-done.2 = bf16[512,512]{1,0:T(8,128)(2,1)} collective-permute-done((bf16[512,512]{1,0:T(8,128)(2,1)S(1)}, bf16[512,512]{1,0:T(8,128)(2,1)}, u32[]{:S(2)}, u32[]{:S(2)}) %collective-permute-start.2) | collective-permute-done | bytes 524320 | tf_op jit(solution)/shard_map/ppermute | solution.py:15
  287.2 3.3 collective-permute-done.3
  290.5 1.6 select_bitcast_fusion.1
  292.1 0.9 copy.71
  293.9 138.7 %all-gather.13.cloned.1.call-done = bf16[5376,1024]{1,0:T(8,128)(2,1)} async-done(((bf16[672,1024]{1,0:T(8,128)(2,1)}), bf16[5376,1024]{1,0:T(8,128)(2,1)}) %all-gather.13.cloned.1.call-update) | async-done | bytes 11010064 | tf_op jit(solution)/shard_map/all_gather | solution.py:60
  432.6 10.2 %convolution_bitcast_fusion = f32[64,8,8,128]{3,1,2,0:T(8,128)S(1)} fusion(bf16[512,5376]{1,0:T(8,128)(2,1)} %all-gather.7.cloned.1.call-done, bf16[5376,1024]{1,0:T(8,128)(2,1)} %all-gather.13.cloned.1.call-done), kind=kOutput, calls=%fused_computation.28 | convolution fusion | flops 5637144576 | bytes 18612224 | tf_op jit(solution)/shard_map/dot_general | solution.py:58
  445.1 1.1 multiply_subtract_fusion
  448.2 11.9 %fusion.15 = f32[4,1536,512,2]{2,1,3,0:T(8,128)} fusion(bf16[512,4,2,128]{3,0,2,1:T(8,128)(2,1)S(1)} %fusion.13, bf16[512,4,128]{2,0,1:T(8,128)(2,1)S(1)} %maximum_convert_fusion, bf16[512,4,128]{2,0,1:T(8,128)(2,1)S(1)} %bitcast.78, bf16[512,4,128]{2,0,1:T(8,128)(2,1)S(1)} %bitcast.80), kind=kOutput, calls=%fused_computation.38 | convolution fusion | flops 1615331328 | bytes 27787264 | tf_op jit(solution)/shard_map/qhgd,khd->hgqk/dot_general | solution.py:98
  460.1 7.9 %fusion.25 = f32[4,2,512]{2,1,0:T(2,128)S(1)} fusion(pred[512,1536]{0,1:T(8,128)(4,1)S(1)} %copy-done.5, bf16[512,4,2,128]{3,0,2,1:T(8,128)(2,1)S(1)} %fusion.13, bf16[512,4,128]{2,0,1:T(8,128)(2,1)S(1)} %maximum_convert_fusion, bf16[512,4,128]{2,0,1:T(8,128)(2,1)S(1)} %bitcast.79, bf16[512,4,128]{2,0,1:T(8,128)(2,1)S(1)} %bitcast.81), kind=kOutput, calls=%fused_computation.63 | convolution fusion | flops 1634207232 | bytes 3424256 | tf_op jit(solution)/shard_map/sub | solution.py:110
  468.0 121.8 %all-gather.15.cloned.1.call-done = bf16[8192,672]{0,1:T(8,128)(2,1)} async-done(((bf16[1024,672]{0,1:T(8,128)(2,1)}), bf16[8192,672]{0,1:T(8,128)(2,1)}) %all-gather.15.cloned.1.call-update) | async-done | bytes 11010064 | tf_op jit(solution)/shard_map/all_gather | solution.py:118
  589.8 10.9 %copy.67 = bf16[84,8,8,1024]{3,2,1,0:T(8,128)(2,1)S(1)} copy(bf16[84,8,8,1024]{3,1,2,0:T(8,128)(2,1)} %bitcast.74) | data formatting | bytes 22020096
  600.6 7.9 %copy.58 = bf16[1024,8,672]{0,2,1:T(8,128)(2,1)} copy(bf16[1024,8,672]{0,1,2:T(8,128)(2,1)S(1)} %bitcast.72) | data formatting | bytes 22020096 | tf_op jit(solution)/shard_map/reshape | solution.py:118
  608.5 12.7 %fusion.14 = bf16[4,128,2,512]{3,1,2,0:T(8,128)(2,1)S(1)} fusion(bf16[1536,4,128,1]{0,2,3,1:T(8,128)(2,1)S(1)} %bitcast.82, f32[4,2,512]{2,1,0:T(2,128)S(1)} %fusion.25, f32[4,1536,512,2]{2,1,3,0:T(8,128)} %fusion.15, pred[512,1536]{0,1:T(8,128)(4,1)S(1)} %copy-done.5), kind=kOutput, calls=%fused_computation.31 | convolution fusion | flops 1636308480 | bytes 28590080 | tf_op jit(solution)/shard_map/hgqk,khd->qhgd/dot_general | solution.py:112
  621.2 12.3 %convolution_convert_fusion = bf16[512,5376]{1,0:T(8,128)(2,1)} fusion(bf16[512,1024]{0,1:T(8,128)(2,1)S(1)} %bitcast.84, bf16[1024,5376]{0,1:T(8,128)(2,1)} %bitcast.75), kind=kOutput, calls=%fused_computation.8 | convolution fusion | flops 5639897088 | bytes 17563648 | tf_op jit(solution)/shard_map/dot_general | solution.py:116
  633.5 51.4 %reduce-scatter.2.cloned.1.call-done = bf16[128,5376]{1,0:T(8,128)(2,1)} async-done(((bf16[512,5376]{1,0:T(8,128)(2,1)}), bf16[128,5376]{1,0:T(8,128)(2,1)}) %reduce-scatter.2.cloned.1.call-update) | async-done | bytes 1376272 | tf_op jit(solution)/shard_map/reduce_scatter | solution.py:121
  684.8 1.7 fusion.7
  686.6 3.0 fusion.12
  (56 shorter events, 9.9 us)
Async XLA Ops:
  6.5 49.3 %all-gather.7.cloned.1.call-start = ((), (), s32[]{:S(2)}) async-start(), calls=%async_computation.1 | async-start | bytes 6881280 | tf_op jit(solution)/shard_map/all_gather | solution.py:52
  11.1 136.1 %all-gather.9.cloned.1.call-start = ((), (), s32[]{:S(2)}) async-start(), calls=%async_computation.2 | async-start | bytes 6193152 | tf_op jit(solution)/shard_map/all_gather | solution.py:62
  11.8 243.2 %all-gather.11.cloned.1.call-start = ((), (), s32[]{:S(2)}) async-start(), calls=%async_computation.3 | async-start | bytes 6193152 | tf_op jit(solution)/shard_map/all_gather | solution.py:61
  12.6 420.0 %all-gather.13.cloned.1.call-start = ((), (), s32[]{:S(2)}) async-start(), calls=%async_computation.4 | async-start | bytes 12386304 | tf_op jit(solution)/shard_map/all_gather | solution.py:60
  13.1 576.6 %all-gather.15.cloned.1.call-start = ((), (), s32[]{:S(2)}) async-start(), calls=%async_computation.6 | async-start | bytes 12386304 | tf_op jit(solution)/shard_map/all_gather | solution.py:118
  13.7 671.1 %reduce-scatter.2.cloned.1.call-start = ((), (), s32[]{:S(2)}) async-start(), calls=%async_computation.5 | async-start | bytes 6881280 | tf_op jit(solution)/shard_map/reduce_scatter | solution.py:121
  155.2 106.9 %copy-start.7 = (f32[128]{0:T(128)S(1)}, f32[128]{0:T(128)}, u32[]{:S(2)}) copy-start(f32[128]{0:T(128)} %param.20) | copy-start | bytes 1540
  155.2 114.8 %collective-permute-start = (bf16[512,512]{1,0:T(8,128)(2,1)}, bf16[512,512]{1,0:T(8,128)(2,1)}, u32[]{:S(2)}, u32[]{:S(2)}) collective-permute-start(bf16[512,512]{1,0:T(8,128)(2,1)} %convolution_convert_fusion.1), channel_id=1, source_target_pairs={{0,8},{4,12},{8,16},{12,20},{16,24},{20,28},{1,9},{5,13},{9,17},{1... | collective-permute-start | bytes 1572872 | tf_op jit(solution)/shard_map/ppermute | solution.py:15
  158.6 111.4 %collective-permute-start.1 = (bf16[512,512]{1,0:T(8,128)(2,1)}, bf16[512,512]{1,0:T(8,128)(2,1)}, u32[]{:S(2)}, u32[]{:S(2)}) collective-permute-start(bf16[512,512]{1,0:T(8,128)(2,1)} %convolution_convert_fusion.1), channel_id=1, source_target_pairs={{0,4},{4,8},{8,12},{12,16},{16,20},{20,24},{24,28},{1,5},{5,9},{9,... | collective-permute-start | bytes 1572872 | tf_op jit(solution)/shard_map/ppermute | solution.py:15
  262.4 7.6 %copy-start.4 = (bf16[1024,512]{1,0:T(8,128)(2,1)S(1)}, bf16[1024,512]{1,0:T(8,128)(2,1)}, u32[]{:S(2)}) copy-start(bf16[1024,512]{1,0:T(8,128)(2,1)} %param.22) | copy-start | bytes 3145732
  263.2 24.0 %collective-permute-start.2 = (bf16[512,512]{1,0:T(8,128)(2,1)S(1)}, bf16[512,512]{1,0:T(8,128)(2,1)}, u32[]{:S(2)}, u32[]{:S(2)}) collective-permute-start(bf16[512,512]{1,0:T(8,128)(2,1)S(1)} %copy_bitcast_fusion), channel_id=1, source_target_pairs={{0,8},{4,12},{8,16},{12,20},{16,24},{20,28},{1,9},{5,13},{9,17},{1... | collective-permute-start | bytes 1572872 | tf_op jit(solution)/shard_map/ppermute | solution.py:15
  266.4 24.0 %collective-permute-start.3 = (bf16[512,512]{1,0:T(8,128)(2,1)S(1)}, bf16[512,512]{1,0:T(8,128)(2,1)}, u32[]{:S(2)}, u32[]{:S(2)}) collective-permute-start(bf16[512,512]{1,0:T(8,128)(2,1)S(1)} %copy_bitcast_fusion), channel_id=1, source_target_pairs={{0,4},{4,8},{8,12},{12,16},{16,20},{20,24},{24,28},{1,5},{5,9},{9,... | collective-permute-start | bytes 1572872 | tf_op jit(solution)/shard_map/ppermute | solution.py:15
  442.8 1.4 copy-start.8
  447.0 1.0 copy-start.1
  447.0 1.2 copy-start.2
  448.2 11.9 %copy-start.5 = (pred[512,1536]{0,1:T(8,128)(4,1)S(1)}, pred[512,1536]{0,1:T(8,128)(4,1)}, u32[]{:S(2)}) copy-start(pred[512,1536]{0,1:T(8,128)(4,1)} %and_and_fusion) | copy-start | bytes 2359300
  600.6 7.9 %copy-start.3 = (bf16[1536,512]{0,1:T(8,128)(2,1)S(1)}, bf16[1536,512]{0,1:T(8,128)(2,1)}, u32[]{:S(2)}) copy-start(bf16[1536,512]{0,1:T(8,128)(2,1)} %copy.62) | copy-start | bytes 4718596
  633.4 53.1 %copy-start = (bf16[128,5376]{1,0:T(8,128)(2,1)S(1)}, bf16[128,5376]{1,0:T(8,128)(2,1)}, u32[]{:S(2)}) copy-start(bf16[128,5376]{1,0:T(8,128)(2,1)} %param.12) | copy-start | bytes 4128772
  633.4 53.1 %copy-start.6 = (f32[5376]{0:T(1024)S(1)}, f32[5376]{0:T(1024)}, u32[]{:S(2)}) copy-start(f32[5376]{0:T(1024)} %param.23) | copy-start | bytes 64516
Sparse Core Ops, SparseCore 0:
  11.2 44.6 all-gather.6
  58.0 89.1 all-gather.8
  149.4 105.6 all-gather.10
  257.0 175.5 all-gather.12
  434.6 155.0 all-gather.14
  633.6 51.2 reduce-scatter.1
